TPU v7x, 32 devices: a whole 2x2x4 slice. The times are simulated.
32 devices in a mesh: energy: 4 (over z), block: 4 (over y, x), role: 2 (over core).
Axes of the slice: x: 2, y: 2, z: 4, core: 2. Of those that a mesh axis runs over, the one named last changes fastest.
Arguments:
- sigma_in: float32 [2, 8, 4, 128, 128], P(None, ('energy', 'role'), 'block'), may hold values from -0.009 to 0.009
- hamiltonian: float32 [4, 128, 128], P('block'), may hold values from -0.5 to 0.5
- coupling: float32 [4, 128, 128], P('block'), may hold values from -0.25 to 0.25
- coulomb: float32 [4, 16384], P('block', ('energy', 'role')), may hold values from 0.2 to 1
- pattern: int32 [2, 4, 4, 4], P(None, 'block'), may hold values 0 or 1
- offsets: int32 [16], replicated, may hold values from 0 to 3
Outputs:
- green: float32 [2, 8, 4, 128, 128], P(None, ('energy', 'role'), 'block')
- sigma_out: float32 [2, 8, 4, 128, 128], P(None, ('energy', 'role'), 'block')
All inputs are finite; a program needn't handle non-finite values. No bound on the sum of `pattern` on one device may be relied on, other than what follows from the above.
Results may differ from a plain program's by a relative error of at most 0.0003.
Values sent between devices are 32-bit elements; how exact they have to be, the bound alone decides.
No kernel may reach another device: no remote copies, remote signals or barrier semaphores. Data moves between devices by JAX's collectives and lax.ppermute only.
A program may use at most 64 MiB of HBM per device.

v0:
```python
import functools

import jax
import jax.numpy as jnp
from jax import lax
from jax.experimental import pallas as pl
from jax.experimental.pallas import tpu as pltpu
from jax.sharding import PartitionSpec as P

ETA = 0.1
CONTACT = 0.5
HIGH = lax.Precision.HIGHEST
F32 = jnp.float32
BF16 = jnp.bfloat16

LOW = 1e-4
STEPS = 8
POLISH = 2
TOL = 1e-6
MAX_SAFE = 300


def step_table(low, steps):
    rows = []
    for _ in range(steps):
        scale = 4.0 / (1.0 + low) ** 2
        rows.append((scale * (1.0 + low), scale))
        low = scale * low
    return rows, 2.0 / (1.0 + low)


def split(value):
    high = value.astype(BF16)
    return high, (value - high.astype(F32)).astype(BF16)


def dot(left, right):
    return jnp.dot(left, right, preferred_element_type=F32)


def dot3(left, right_high, right_low):
    left_high, left_low = split(left)
    return dot(left_high, right_high) + (dot(left_high, right_low) + dot(left_low, right_high))


def embed(wide):
    half = wide.shape[1] // 2
    return jnp.concatenate(
        [wide, jnp.concatenate([-wide[:, half:], wide[:, :half]], axis=1)], axis=0
    )


def embed_split(wide):
    high, low = split(wide)
    return embed(high), embed(low)


def wide_eye(size):
    row = lax.broadcasted_iota(jnp.int32, (size, 2 * size), 0)
    col = lax.broadcasted_iota(jnp.int32, (size, 2 * size), 1)
    return jnp.where(row == col, 1.0, 0.0).astype(F32)


def adjoint(wide):
    half = wide.shape[1] // 2
    return jnp.concatenate([wide[:, :half].T, -wide[:, half:].T], axis=1)


def invert_many(slots, s_ref, x_ref, z_ref, eh_ref, el_ref):
    size = s_ref.shape[1]
    eye = wide_eye(size)
    table, last = step_table(LOW, STEPS)
    alphas = {}
    for slot in slots:
        value = s_ref[slot]
        high, low = embed_split(value)
        eh_ref[slot] = high
        el_ref[slot] = low
        normal = dot3(adjoint(value), high, low)
        magnitude = jnp.abs(normal[:, :size]) + jnp.abs(normal[:, size:])
        bound = jnp.max(jnp.sum(magnitude, axis=1, keepdims=True), axis=0, keepdims=True)
        alpha = 1.0 / bound
        alphas[slot] = alpha
        first = normal * alpha
        z_ref[slot, :size] = first
        z_ref[slot, size:] = eye
    for index in range(STEPS):
        lift, scale = table[index]
        for slot in slots:
            both = z_ref[slot]
            high, low = embed_split(both[:size])
            z_ref[slot] = lift * both - scale * dot3(both, high, low)
    for slot in slots:
        value = s_ref[slot]
        high, low = embed_split(adjoint(value))
        x_ref[slot] = (last * alphas[slot]) * dot3(z_ref[slot, size:], high, low)
    worst = None
    for _ in range(POLISH):
        worst = None
        for slot in slots:
            approx = x_ref[slot]
            rest = eye - dot3(approx, eh_ref[slot], el_ref[slot])
            high, low = embed_split(approx)
            x_ref[slot] = approx + dot3(rest, high, low)
            size_rest = jnp.sum(rest * rest)
            worst = size_rest if worst is None else jnp.maximum(worst, size_rest)

    @pl.when(jnp.logical_not(worst < TOL))
    def _():
        for slot in slots:
            x_ref[slot] = adjoint(s_ref[slot]) * alphas[slot]

        def unfinished(state):
            return jnp.logical_and(state[0] < MAX_SAFE, jnp.logical_not(state[1] < TOL))

        def refine(state):
            worst = None
            for slot in slots:
                approx = x_ref[slot]
                rest = eye - dot3(approx, eh_ref[slot], el_ref[slot])
                high, low = embed_split(approx)
                x_ref[slot] = approx + dot3(rest, high, low)
                size_rest = jnp.sum(rest * rest)
                worst = size_rest if worst is None else jnp.maximum(worst, size_rest)
            return state[0] + 1, worst

        lax.while_loop(unfinished, refine, (jnp.int32(0), jnp.float32(1e30)))


def prepare_kernel(total, last_block, pattern_ref, sigma_ref, ham_ref, coupling_ref, coulomb_ref, out_ref, weight_ref):
    size = ham_ref.shape[-1]
    tiles = pattern_ref.shape[-1]
    tile = size // tiles
    block = lax.axis_index("block")
    place = lax.axis_index("energy") * lax.axis_size("role") + lax.axis_index("role")

    def mask_rows(which, row_tile):
        lane = lax.broadcasted_iota(jnp.int32, (1, size), 1) // tile
        row = jnp.zeros((1, size), F32)
        for column in range(tiles):
            row = jnp.where(lane == column, pattern_ref[which, 0, row_tile, column].astype(F32), row)
        return row

    mask = jnp.concatenate(
        [jnp.broadcast_to(mask_rows(0, row_tile), (tile, size)) for row_tile in range(tiles)], axis=0
    )
    masked = ham_ref[0] * mask
    onsite = 0.5 * (masked + masked.T)
    row = lax.broadcasted_iota(jnp.int32, (size, size), 0)
    col = lax.broadcasted_iota(jnp.int32, (size, size), 1)
    number = jnp.full((size, size), place, jnp.int32).astype(F32)
    energy = -3.0 + 6.0 * number / total
    out_ref[0] = jnp.where(row == col, energy, 0.0) - onsite - sigma_ref[0, 0, 0]
    out_ref[1] = jnp.where(row == col, ETA, 0.0) - sigma_ref[1, 0, 0]
    out_ref[2] = coupling_ref[0]

    @pl.when(block == last_block)
    def _():
        square = jnp.dot(
            coupling_ref[0].T, coupling_ref[0], precision=HIGH, preferred_element_type=F32
        )
        out_ref[1] += CONTACT * square

    rows = coulomb_ref.shape[0]
    for local_row in range(rows):
        tile_row = (place * rows + local_row) // tile
        lane = lax.broadcasted_iota(jnp.int32, (1, size), 1) // tile
        line = jnp.zeros((1, size), F32)
        for column in range(tiles):
            line = jnp.where(lane == column, pattern_ref[1, 0, tile_row, column].astype(F32), line)
        value = coulomb_ref[local_row : local_row + 1] * line
        weight_ref[local_row : local_row + 1] = value * value


def green_kernel(groups, all_ref, out_ref, pieces_ref, s_ref, x_ref, z_ref, eh_ref, el_ref, k_ref):
    size = all_ref.shape[-1]
    own = lax.axis_index("block")
    far = own ^ 2
    low_half = own % 2 == 0
    middle = jnp.where(low_half, 1, 2)
    other = jnp.where(low_half, 3, 0)

    def base(block):
        return jnp.concatenate([all_ref[block, 0], all_ref[block, 1]], axis=1)

    for block in range(3):
        value = all_ref[block, 2]
        k_ref[block] = value
        k_ref[3 + block] = value.T

    def link(source, target):
        return k_ref[jnp.where(target > source, source, 3 + target)]

    s_ref[0] = base(middle)
    s_ref[1] = base(other)
    invert_many((0, 1), s_ref, x_ref, z_ref, eh_ref, el_ref)

    beside = jnp.where(low_half, 2, 1)
    to_other = link(beside, other)
    both = jnp.concatenate([link(own, middle), link(far, middle)], axis=0)
    both_t = jnp.concatenate([link(middle, own), link(middle, far)], axis=1)

    def congruence(left, value, right):
        high, low = split(value)
        first = dot3(left, high, low)
        rows = jnp.concatenate([first[:, :size], first[:, size:]], axis=0)
        high, low = split(right)
        result = dot3(rows, high, low)
        count = left.shape[0]
        return result[:count], result[count:]

    real, imag = congruence(both, x_ref[0], both_t)
    o_real, o_imag = congruence(to_other, x_ref[1], link(other, beside))
    side = jnp.concatenate([o_real, o_imag], axis=1)
    beside_far = beside == far

    def wide(rows, columns):
        return jnp.concatenate([real[rows, columns], imag[rows, columns]], axis=1)

    top, bottom = slice(0, size), slice(size, 2 * size)
    s_ref[0] = base(far) - wide(bottom, bottom) - jnp.where(beside_far, side, 0.0)
    own_part = base(own) - wide(top, top) - jnp.where(beside_far, 0.0, side)
    up = wide(top, bottom)
    down = wide(bottom, top)
    s_ref[1] = own_part
    z_ref[1, :size] = up
    z_ref[1, size:] = down
    invert_many((0,), s_ref, x_ref, z_ref, eh_ref, el_ref)
    high, low = embed_split(x_ref[0])
    first = dot3(z_ref[1, :size], high, low)
    high, low = embed_split(z_ref[1, size:])
    s_ref[0] = s_ref[1] - dot3(first, high, low)
    invert_many((0,), s_ref, x_ref, z_ref, eh_ref, el_ref)
    result = x_ref[0]
    out_ref[0, 0, 0] = result[:, :size]
    out_ref[1, 0, 0] = result[:, size:]
    rows = size // groups
    for group in range(groups):
        part = slice(group * rows, (group + 1) * rows)
        pieces_ref[group, 0] = result[part, :size]
        pieces_ref[group, 1] = result[part, size:]


def screen_kernel(offsets_ref, weight_ref, g_ref, out_ref):
    energies = g_ref.shape[0]
    count = offsets_ref.shape[0]
    factor = 6.0 / energies / (2.0 * 3.141592653589793) / count
    weight = weight_ref[...]

    def uses(offset):
        return lax.fori_loop(
            0, count, lambda i, total: total + jnp.where(offsets_ref[i] == offset, 1, 0), jnp.int32(0)
        )

    if energies <= 16:
        real = [g_ref[n, 0] for n in range(energies)]
        imag = [g_ref[n, 1] for n in range(energies)]
        out_real = [jnp.zeros_like(weight) for _ in range(energies)]
        out_imag = [jnp.zeros_like(weight) for _ in range(energies)]
        hits = [jnp.int32(0) for _ in range(energies)]
        for index in range(count):
            offset = offsets_ref[index]
            for d in range(energies):
                hits[d] = hits[d] + jnp.where(offset == d, 1, 0)
        for d in range(energies):
            scale = weight * (factor * hits[d].astype(F32))
            p_real = jnp.zeros_like(weight)
            p_imag = jnp.zeros_like(weight)
            for n in range(d, energies):
                p_real += real[n] * real[n - d] - imag[n] * imag[n - d]
                p_imag += real[n] * imag[n - d] + imag[n] * real[n - d]
            p_real *= scale
            p_imag *= scale
            for n in range(d, energies):
                out_real[n] += real[n - d] * p_real - imag[n - d] * p_imag
                out_imag[n] += real[n - d] * p_imag + imag[n - d] * p_real
        for n in range(energies):
            out_ref[n, 0] = out_real[n]
            out_ref[n, 1] = out_imag[n]
    else:
        out_ref[...] = jnp.zeros_like(out_ref)

        @pl.loop(0, energies)
        def _(d):
            hits = uses(d)

            @pl.when(hits > 0)
            def _():
                scale = weight * (factor * hits.astype(F32))

                def gather(n, total):
                    a, b, c, e = g_ref[n, 0], g_ref[n, 1], g_ref[n - d, 0], g_ref[n - d, 1]
                    return total[0] + a * c - b * e, total[1] + a * e + b * c

                zero = jnp.zeros_like(weight)
                p_real, p_imag = lax.fori_loop(d, energies, gather, (zero, zero))
                p_real, p_imag = p_real * scale, p_imag * scale

                @pl.loop(d, energies)
                def _(n):
                    a, b = g_ref[n - d, 0], g_ref[n - d, 1]
                    out_ref[n, 0] += a * p_real - b * p_imag
                    out_ref[n, 1] += a * p_imag + b * p_real


VM = pl.BlockSpec(memory_space=pltpu.VMEM)
SM = pl.BlockSpec(memory_space=pltpu.SMEM)


def body(sigma_in, hamiltonian, coupling, coulomb, pattern, offsets):
    size = hamiltonian.shape[-1]
    blocks = lax.axis_size("block")
    groups = lax.axis_size("energy") * lax.axis_size("role")
    rows = size // groups
    assert blocks == 4 and sigma_in.shape[1] == 1
    packed, weight = pl.pallas_call(
        functools.partial(prepare_kernel, groups, blocks - 1),
        out_shape=(
            jax.ShapeDtypeStruct((3, size, size), F32),
            jax.ShapeDtypeStruct((rows, size), F32),
        ),
        in_specs=[SM, VM, VM, VM, VM],
        out_specs=(VM, VM),
        name="prepare",
    )(pattern, sigma_in, hamiltonian, coupling, coulomb.reshape(rows, size))
    gathered = lax.all_gather(packed, "block", axis=0, tiled=False)
    green, pieces = pl.pallas_call(
        functools.partial(green_kernel, groups),
        out_shape=(
            jax.ShapeDtypeStruct((2, 1, 1, size, size), F32),
            jax.ShapeDtypeStruct((groups, 2, rows, size), F32),
        ),
        in_specs=[VM],
        out_specs=(VM, VM),
        scratch_shapes=[
            pltpu.VMEM((2, size, 2 * size), F32),
            pltpu.VMEM((2, size, 2 * size), F32),
            pltpu.VMEM((2, 2 * size, 2 * size), F32),
            pltpu.VMEM((2, 2 * size, 2 * size), BF16),
            pltpu.VMEM((2, 2 * size, 2 * size), BF16),
            pltpu.VMEM((6, size, size), F32),
        ],
        name="green",
    )(gathered)
    spread = lax.all_to_all(pieces, ("energy", "role"), split_axis=0, concat_axis=0, tiled=True)
    screened = pl.pallas_call(
        screen_kernel,
        out_shape=jax.ShapeDtypeStruct(spread.shape, F32),
        in_specs=[SM, VM, VM],
        out_specs=VM,
        name="screen",
    )(offsets, weight, spread)
    returned = lax.all_to_all(screened, ("energy", "role"), split_axis=0, concat_axis=0, tiled=True)
    sigma_out = returned.transpose(1, 0, 2, 3).reshape(2, 1, 1, size, size)
    return green, sigma_out


def solution(mesh):
    in_specs = (
        P(None, ("energy", "role"), "block", None, None),
        P("block", None, None),
        P("block", None, None),
        P("block", ("energy", "role")),
        P(None, "block", None, None),
        P(),
    )
    out_specs = (
        P(None, ("energy", "role"), "block", None, None),
        P(None, ("energy", "role"), "block", None, None),
    )
    return jax.shard_map(body, mesh=mesh, in_specs=in_specs, out_specs=out_specs, check_vma=False)
```

profile of v0, /device:TPU:0, one launch (start us, length us, event | category | flops | bytes accessed | tf_op | source)
XLA Modules:
  0.0 78.4 jit_solution(214452419304322469)
XLA Ops:
  0.6 1.9 %prepare.1 = (f32[3,128,128]{2,1,0:T(8,128)}, f32[16,128]{1,0:T(8,128)}) custom-call(s32[2,1,4,4]{3,2,1,0:T(4,128)} %pattern_ref.1, f32[2,1,1,128,128]{4,3,2,1,0:T(8,128)} %sigma_ref.1, f32[1,128,128]{2,1,0:T(8,128)} %ham_ref.1, f32[1,128,128]{2,1,0:T(8,128)} %coupling_ref.1, f32[16,128]{1,0:T(8,128)} %bitcast.9), custom_call_target="tpu_custom_call" | custom-call | tf_op jit(solution)/shard_map/prepare/pallas_call | solution.py:316
  2.5 16.1 %all-gather = f32[12,128,128]{2,1,0:T(8,128)} all-gather(f32[3,128,128]{2,1,0:T(8,128)} %get-tuple-element.6), channel_id=2, replica_groups=mesh['energy'=4,'block'=4,'role'=2] {'block'}, dimensions={0}, use_global_device_ids=true | all-gather | bytes 983040 | tf_op jit(solution)/shard_map/all_gather | solution.py:326
  18.6 24.5 %green.1 = (f32[2,1,1,128,128]{4,3,2,1,0:T(8,128)}, f32[8,2,16,128]{3,2,1,0:T(8,128)}) custom-call(f32[4,3,128,128]{3,2,1,0:T(8,128)} %bitcast.6), custom_call_target="tpu_custom_call" | custom-call | tf_op jit(solution)/shard_map/green/pallas_call | solution.py:327
  43.1 22.9 %all_to_all.10.g_ref = f32[8,2,16,128]{3,2,1,0:T(8,128)} all-to-all(f32[8,2,16,128]{3,2,1,0:T(8,128)} %get-tuple-element.9), channel_id=1, replica_groups=mesh['energy'=4,'block'=4,'role'=2] {'energy','role'}, dimensions={0} | all-to-all | bytes 262144 | tf_op jit(solution)/shard_map/all_to_all | solution.py:345
  66.0 1.7 %screen.1 = f32[8,2,16,128]{3,2,1,0:T(8,128)} custom-call(s32[16]{0:T(128)} %offsets_ref.1, f32[16,128]{1,0:T(8,128)} %get-tuple-element.8.weight_ref, f32[8,2,16,128]{3,2,1,0:T(8,128)} %all_to_all.10.g_ref), custom_call_target="tpu_custom_call" | custom-call | tf_op jit(solution)/shard_map/screen/pallas_call | solution.py:346
  67.7 10.0 %all_to_all.11 = f32[8,2,16,128]{3,2,1,0:T(8,128)S(1)} all-to-all(f32[8,2,16,128]{3,2,1,0:T(8,128)} %screen.1), channel_id=1, replica_groups=mesh['energy'=4,'block'=4,'role'=2] {'energy','role'}, dimensions={0} | all-to-all | bytes 262144 | tf_op jit(solution)/shard_map/all_to_all | solution.py:353
  77.8 0.7 copy.10
where the time goes:
time: 78.9 us; the launch traced here: 78.4 us
  blocking collectives  49 us (62%)
  Pallas kernels  28.1 us (36%)
    pallas_call x1, Pallas kernels, body(): pl.pallas_call(functools.partial(green_kernel, groups), out_shape=(jax.Sh...  24.5 us
    all_to_all x1, blocking collectives, body(): lax.all_to_all(pieces, ('energy', 'role'), split_axis=0, concat_axis=0, t...  22.9 us
    all_gather x1, blocking collectives, body(): gathered = lax.all_gather(packed, 'block', axis=0, tiled=False)  16.1 us
    all_to_all x1, blocking collectives, body(): lax.all_to_all(screened, ('energy', 'role'), split_axis=0, concat_axis=0,...  10 us
    pallas_call x1, Pallas kernels, body(): pl.pallas_call(functools.partial(prepare_kernel, groups, blocks - 1), out...  1.87 us
    pallas_call x1, Pallas kernels, body(): pl.pallas_call(screen_kernel, out_shape=jax.ShapeDtypeStruct(spread.shape...  1.74 us

commit v1 on v0

--- a/solution.py
+++ b/solution.py
@@ -13,9 +13,9 @@
 F32 = jnp.float32
 BF16 = jnp.bfloat16
 
-LOW = 1e-4
-STEPS = 8
-POLISH = 2
+LOW = 4e-4
+STEPS = 7
+TRUST = 2e-5
 TOL = 1e-6
 MAX_SAFE = 300
 
@@ -38,9 +38,8 @@
     return jnp.dot(left, right, preferred_element_type=F32)
 
 
-def dot3(left, right_high, right_low):
-    left_high, left_low = split(left)
-    return dot(left_high, right_high) + (dot(left_high, right_low) + dot(left_low, right_high))
+def dot3(left, right):
+    return dot(left[0], right[0]) + (dot(left[0], right[1]) + dot(left[1], right[0]))
 
 
 def embed(wide):
@@ -50,9 +49,8 @@
     )
 
 
-def embed_split(wide):
-    high, low = split(wide)
-    return embed(high), embed(low)
+def embed_both(parts):
+    return embed(parts[0]), embed(parts[1])
 
 
 def wide_eye(size):
@@ -66,62 +64,72 @@
     return jnp.concatenate([wide[:, :half].T, -wide[:, half:].T], axis=1)
 
 
-def invert_many(slots, s_ref, x_ref, z_ref, eh_ref, el_ref):
+def invert_many(slots, s_ref, x_ref, t_ref, e_ref, alpha_ref):
     size = s_ref.shape[1]
-    eye = wide_eye(size)
     table, last = step_table(LOW, STEPS)
-    alphas = {}
     for slot in slots:
         value = s_ref[slot]
-        high, low = embed_split(value)
-        eh_ref[slot] = high
-        el_ref[slot] = low
-        normal = dot3(adjoint(value), high, low)
-        magnitude = jnp.abs(normal[:, :size]) + jnp.abs(normal[:, size:])
-        bound = jnp.max(jnp.sum(magnitude, axis=1, keepdims=True), axis=0, keepdims=True)
-        alpha = 1.0 / bound
-        alphas[slot] = alpha
-        first = normal * alpha
-        z_ref[slot, :size] = first
-        z_ref[slot, size:] = eye
+        parts = split(value)
+        e_ref[slot, 0], e_ref[slot, 1] = embed_both(parts)
+        turned = adjoint(value)
+        x_ref[slot] = turned
+        t_ref[slot] = dot3(parts, embed_both(split(turned)))
     for index in range(STEPS):
         lift, scale = table[index]
         for slot in slots:
-            both = z_ref[slot]
-            high, low = embed_split(both[:size])
-            z_ref[slot] = lift * both - scale * dot3(both, high, low)
+            power = t_ref[slot]
+            approx = x_ref[slot]
+            parts = split(power)
+            weights = embed_both(parts)
+            if index == 0:
+                size_of = jnp.abs(power[:, :size]) + jnp.abs(power[:, size:])
+                bound = jnp.max(jnp.sum(size_of, axis=0, keepdims=True), axis=1, keepdims=True)
+                alpha = jnp.broadcast_to(1.0 / bound, (1, 2 * size))
+                alpha_ref[slot] = alpha
+                t_ref[slot] = (lift * alpha) * power - (scale * alpha * alpha) * dot3(parts, weights)
+                x_ref[slot] = (lift * alpha) * approx - (scale * alpha * alpha) * dot3(
+                    split(approx), weights
+                )
+            elif index < STEPS - 1:
+                t_ref[slot] = lift * power - scale * dot3(parts, weights)
+                x_ref[slot] = lift * approx - scale * dot3(split(approx), weights)
+            else:
+                x_ref[slot] = (last * lift) * approx - (last * scale) * dot(
+                    approx.astype(BF16), weights[0]
+                )
+    trusted = None
+    contracting = None
     for slot in slots:
-        value = s_ref[slot]
-        high, low = embed_split(adjoint(value))
-        x_ref[slot] = (last * alphas[slot]) * dot3(z_ref[slot, size:], high, low)
-    worst = None
-    for _ in range(POLISH):
-        worst = None
-        for slot in slots:
-            approx = x_ref[slot]
-            rest = eye - dot3(approx, eh_ref[slot], el_ref[slot])
-            high, low = embed_split(approx)
-            x_ref[slot] = approx + dot3(rest, high, low)
-            size_rest = jnp.sum(rest * rest)
-            worst = size_rest if worst is None else jnp.maximum(worst, size_rest)
-
-    @pl.when(jnp.logical_not(worst < TOL))
+        approx = x_ref[slot]
+        parts = split(approx)
+        rest = wide_eye(size) - dot3(parts, (e_ref[slot, 0], e_ref[slot, 1]))
+        rest_parts = split(rest)
+        square = dot(rest_parts[0], embed(rest_parts[0]))
+        better = approx + dot3(rest_parts, embed_both(parts))
+        x_ref[slot] = better + dot(square.astype(BF16), embed(better.astype(BF16)))
+        good = jnp.sum(square * square) < TRUST
+        near = jnp.sum(rest * rest) < 0.5
+        trusted = good if trusted is None else jnp.logical_and(trusted, good)
+        contracting = near if contracting is None else jnp.logical_and(contracting, near)
+
+    @pl.when(jnp.logical_not(trusted))
     def _():
-        for slot in slots:
-            x_ref[slot] = adjoint(s_ref[slot]) * alphas[slot]
+        @pl.when(jnp.logical_not(contracting))
+        def _():
+            for slot in slots:
+                x_ref[slot] = adjoint(s_ref[slot]) * alpha_ref[slot]
 
         def unfinished(state):
             return jnp.logical_and(state[0] < MAX_SAFE, jnp.logical_not(state[1] < TOL))
 
         def refine(state):
-            worst = None
+            worst = jnp.float32(0.0)
             for slot in slots:
                 approx = x_ref[slot]
-                rest = eye - dot3(approx, eh_ref[slot], el_ref[slot])
-                high, low = embed_split(approx)
-                x_ref[slot] = approx + dot3(rest, high, low)
-                size_rest = jnp.sum(rest * rest)
-                worst = size_rest if worst is None else jnp.maximum(worst, size_rest)
+                parts = split(approx)
+                rest = wide_eye(size) - dot3(parts, (e_ref[slot, 0], e_ref[slot, 1]))
+                x_ref[slot] = approx + dot3(split(rest), embed_both(parts))
+                worst = worst + jnp.sum(rest * rest)
             return state[0] + 1, worst
 
         lax.while_loop(unfinished, refine, (jnp.int32(0), jnp.float32(1e30)))
@@ -172,7 +180,7 @@
         weight_ref[local_row : local_row + 1] = value * value
 
 
-def green_kernel(groups, all_ref, out_ref, pieces_ref, s_ref, x_ref, z_ref, eh_ref, el_ref, k_ref):
+def green_kernel(groups, all_ref, out_ref, pieces_ref, s_ref, x_ref, t_ref, e_ref, alpha_ref, k_ref, up_ref):
     size = all_ref.shape[-1]
     own = lax.axis_index("block")
     far = own ^ 2
@@ -193,7 +201,7 @@
 
     s_ref[0] = base(middle)
     s_ref[1] = base(other)
-    invert_many((0, 1), s_ref, x_ref, z_ref, eh_ref, el_ref)
+    invert_many((0, 1), s_ref, x_ref, t_ref, e_ref, alpha_ref)
 
     beside = jnp.where(low_half, 2, 1)
     to_other = link(beside, other)
@@ -201,11 +209,9 @@
     both_t = jnp.concatenate([link(middle, own), link(middle, far)], axis=1)
 
     def congruence(left, value, right):
-        high, low = split(value)
-        first = dot3(left, high, low)
+        first = dot3(split(left), split(value))
         rows = jnp.concatenate([first[:, :size], first[:, size:]], axis=0)
-        high, low = split(right)
-        result = dot3(rows, high, low)
+        result = dot3(split(rows), split(right))
         count = left.shape[0]
         return result[:count], result[count:]
 
@@ -220,17 +226,13 @@
     top, bottom = slice(0, size), slice(size, 2 * size)
     s_ref[0] = base(far) - wide(bottom, bottom) - jnp.where(beside_far, side, 0.0)
     own_part = base(own) - wide(top, top) - jnp.where(beside_far, 0.0, side)
-    up = wide(top, bottom)
-    down = wide(bottom, top)
+    up_ref[0] = wide(top, bottom)
+    up_ref[1] = wide(bottom, top)
     s_ref[1] = own_part
-    z_ref[1, :size] = up
-    z_ref[1, size:] = down
-    invert_many((0,), s_ref, x_ref, z_ref, eh_ref, el_ref)
-    high, low = embed_split(x_ref[0])
-    first = dot3(z_ref[1, :size], high, low)
-    high, low = embed_split(z_ref[1, size:])
-    s_ref[0] = s_ref[1] - dot3(first, high, low)
-    invert_many((0,), s_ref, x_ref, z_ref, eh_ref, el_ref)
+    invert_many((0,), s_ref, x_ref, t_ref, e_ref, alpha_ref)
+    first = dot3(split(up_ref[0]), embed_both(split(x_ref[0])))
+    s_ref[0] = s_ref[1] - dot3(split(first), embed_both(split(up_ref[1])))
+    invert_many((0,), s_ref, x_ref, t_ref, e_ref, alpha_ref)
     result = x_ref[0]
     out_ref[0, 0, 0] = result[:, :size]
     out_ref[1, 0, 0] = result[:, size:]
@@ -335,10 +337,11 @@
         scratch_shapes=[
             pltpu.VMEM((2, size, 2 * size), F32),
             pltpu.VMEM((2, size, 2 * size), F32),
-            pltpu.VMEM((2, 2 * size, 2 * size), F32),
-            pltpu.VMEM((2, 2 * size, 2 * size), BF16),
-            pltpu.VMEM((2, 2 * size, 2 * size), BF16),
+            pltpu.VMEM((2, size, 2 * size), F32),
+            pltpu.VMEM((2, 2, 2 * size, 2 * size), BF16),
+            pltpu.VMEM((2, 1, 2 * size), F32),
             pltpu.VMEM((6, size, size), F32),
+            pltpu.VMEM((2, size, 2 * size), F32),
         ],
         name="green",
     )(gathered)

time: 78.9 us -> 60.4 us (0.77)
  the two profiles are of different devices: /device:TPU:0 before, /device:TPU:4 now
where the time goes in v1:
time: 60.4 us; the launch traced here: 59.9 us
  blocking collectives  43.1 us (71%)
  Pallas kernels  15.5 us (26%)
  local copies, waits for them, and re-layouts  0.66 us (1%)
  between operations  0.63 us (1%)
    all_to_all x1, blocking collectives, body(): lax.all_to_all(pieces, ('energy', 'role'), split_axis=0, concat_axis=0, t...  19.7 us
    all_gather x1, blocking collectives, body(): gathered = lax.all_gather(packed, 'block', axis=0, tiled=False)  13.4 us
    pallas_call x1, Pallas kernels, body(): pl.pallas_call(functools.partial(green_kernel, groups), out_shape=(jax.Sh...  11.9 us
    all_to_all x1, blocking collectives, body(): lax.all_to_all(screened, ('energy', 'role'), split_axis=0, concat_axis=0,...  10 us
    pallas_call x1, Pallas kernels, body(): pl.pallas_call(functools.partial(prepare_kernel, groups, blocks - 1), out...  1.87 us
    pallas_call x1, Pallas kernels, body(): pl.pallas_call(screen_kernel, out_shape=jax.ShapeDtypeStruct(spread.shape...  1.74 us

profile of v1, /device:TPU:4, one launch (start us, length us, event | category | flops | bytes accessed | tf_op | source)
XLA Modules:
  0.0 59.9 jit_solution(16850963723260285645)
XLA Ops:
  0.6 1.9 %prepare.1 = (f32[3,128,128]{2,1,0:T(8,128)}, f32[16,128]{1,0:T(8,128)}) custom-call(s32[2,1,4,4]{3,2,1,0:T(4,128)} %pattern_ref.1, f32[2,1,1,128,128]{4,3,2,1,0:T(8,128)} %sigma_ref.1, f32[1,128,128]{2,1,0:T(8,128)} %ham_ref.1, f32[1,128,128]{2,1,0:T(8,128)} %coupling_ref.1, f32[16,128]{1,0:T(8,128)} %bitcast.9), custom_call_target="tpu_custom_call" | custom-call | tf_op jit(solution)/shard_map/prepare/pallas_call | solution.py:318
  2.5 13.4 %all-gather = f32[12,128,128]{2,1,0:T(8,128)} all-gather(f32[3,128,128]{2,1,0:T(8,128)} %get-tuple-element.6), channel_id=2, replica_groups=mesh['energy'=4,'block'=4,'role'=2] {'block'}, dimensions={0}, use_global_device_ids=true | all-gather | bytes 983040 | tf_op jit(solution)/shard_map/all_gather | solution.py:328
  15.9 11.9 %green.1 = (f32[2,1,1,128,128]{4,3,2,1,0:T(8,128)}, f32[8,2,16,128]{3,2,1,0:T(8,128)}) custom-call(f32[4,3,128,128]{3,2,1,0:T(8,128)} %bitcast.6), custom_call_target="tpu_custom_call" | custom-call | tf_op jit(solution)/shard_map/green/pallas_call | solution.py:329
  27.8 19.7 %all_to_all.10.g_ref = f32[8,2,16,128]{3,2,1,0:T(8,128)} all-to-all(f32[8,2,16,128]{3,2,1,0:T(8,128)} %get-tuple-element.9), channel_id=1, replica_groups=mesh['energy'=4,'block'=4,'role'=2] {'energy','role'}, dimensions={0} | all-to-all | bytes 262144 | tf_op jit(solution)/shard_map/all_to_all | solution.py:348
  47.4 1.7 %screen.1 = f32[8,2,16,128]{3,2,1,0:T(8,128)} custom-call(s32[16]{0:T(128)} %offsets_ref.1, f32[16,128]{1,0:T(8,128)} %get-tuple-element.8.weight_ref, f32[8,2,16,128]{3,2,1,0:T(8,128)} %all_to_all.10.g_ref), custom_call_target="tpu_custom_call" | custom-call | tf_op jit(solution)/shard_map/screen/pallas_call | solution.py:349
  49.2 10.0 %all_to_all.11 = f32[8,2,16,128]{3,2,1,0:T(8,128)S(1)} all-to-all(f32[8,2,16,128]{3,2,1,0:T(8,128)} %screen.1), channel_id=1, replica_groups=mesh['energy'=4,'block'=4,'role'=2] {'energy','role'}, dimensions={0} | all-to-all | bytes 262144 | tf_op jit(solution)/shard_map/all_to_all | solution.py:356
  59.2 0.7 %copy.10 = f32[2,8,16,128]{3,2,1,0:T(8,128)} copy(f32[2,8,16,128]{3,2,0,1:T(8,128)S(1)} %bitcast.7) | data formatting | bytes 262144 | tf_op jit(solution)/shard_map/transpose | solution.py:357
